TPU v7x, 128 devices: a whole 4x4x4 slice. The times are simulated.
128 devices in a mesh: time: 16 (over z, y_lo, core), chan: 8 (over y_hi, x).
Axes of the slice: x: 4, y: 4 (y_hi: 2, y_lo: 2; y = y_hi * 2 + y_lo), z: 4, core: 2. Of those that a mesh axis runs over, the one named last changes fastest.
Arguments:
- fade_rate: float32 [1, 8192, 4096], P(None, 'time', 'chan'), may hold values from 0.2 to 2
- update_in: bfloat16 [1, 8192, 4096], P(None, 'time', 'chan'), may hold values from -6 to 6
- norm_gain: float32 [4096], P('chan'), may hold values from 0.25 to 1.75
Outputs:
- mixed_out: bfloat16 [1, 8192, 4096], P(None, 'time', 'chan')
All inputs are finite; a program needn't handle non-finite values.
Results may differ from a plain program's by a relative error of at most 0.001.
Values sent between devices are 32-bit elements; how exact they have to be, the bound alone decides.
No kernel may reach another device: no remote copies, remote signals or barrier semaphores. Data moves between devices by JAX's collectives and lax.ppermute only.
A program may use at most 64 MiB of HBM per device.

v0:
```python
import jax
import jax.numpy as jnp
from jax import lax
from jax.sharding import Mesh
from jax.sharding import PartitionSpec as P

CHAN = ("chan_0", "chan_1")


def entering(value, axis, join, neutral):
    count, mine = (lax.axis_size(axis), lax.axis_index(axis))
    pieces = jax.tree.map(lambda part: lax.all_gather(part, axis), value)
    so_far = jax.tree.map(
        lambda part, zero: jnp.full_like(part, 0) + jnp.asarray(zero, part.dtype), value, neutral
    )

    def entering_step(position, so_far):
        longer = join(so_far, jax.tree.map(lambda part: part[position], pieces))
        return jax.tree.map(lambda new, old: jnp.where(position < mine, new, old), longer, so_far)

    return lax.fori_loop(0, count - 1, entering_step, so_far)


def gathered_once(array, axis):
    leaves = jax.tree.leaves(array)
    sequence = sorted(range(len(leaves)), key=lambda k: -leaves[k].size)
    width = (1, *leaves[sequence[0]].shape)[-1]
    lines = [
        jnp.pad(leaves[k].reshape(-1), (0, -leaves[k].size % width)).reshape(-1, width)
        for k in sequence
    ]
    both, at, found = (lax.all_gather(jnp.concatenate(lines), axis), 0, {})
    for k, line in zip(sequence, lines):
        section = both[:, at : at + len(line)].reshape(len(both), -1)
        found[k] = section[:, : leaves[k].size].reshape(-1, *leaves[k].shape)
        at += len(line)
    numbers = iter(range(len(leaves)))
    return jax.tree.map(lambda _: found[next(numbers)], array)


def carried_in(value, axis, join, neutral):
    count, mine = (lax.axis_size(axis), lax.axis_index(axis))
    pieces = gathered_once(value, axis)
    pieces = jax.tree.map(lambda part: part[::-1], pieces)
    mine = count - 1 - mine
    so_far = jax.tree.map(
        lambda part, zero: jnp.full_like(part, 0) + jnp.asarray(zero, part.dtype), value, neutral
    )

    def carried_step(position, so_far):
        longer = join(so_far, jax.tree.map(lambda part: part[position], pieces))
        return jax.tree.map(lambda new, old: jnp.where(position < mine, new, old), longer, so_far)

    return lax.fori_loop(0, count - 1, carried_step, so_far)


def over_axes(array, axes):
    for axis in axes:
        array = lax.psum(array, axis)
    return array


def join_pair(earlier, later):
    return (earlier[0] * later[0], later[0] * earlier[1] + later[1])


def per_device(fade_rate, update_in, norm_gain):
    total_length = fade_rate.shape[1] * lax.axis_size("time")
    keep = jnp.exp(-fade_rate / total_length)
    push = update_in.astype(jnp.float32) * total_length ** (-0.5)
    product, forward = lax.associative_scan(join_pair, (keep, push), axis=1)
    entering_forward = entering(
        (product[:, -1], forward[:, -1]),
        "time",
        join_pair,
        (jnp.ones_like(keep[:, 0]), jnp.zeros_like(push[:, 0])),
    )
    forward = forward + product * entering_forward[1][:, None]
    product, backward = lax.associative_scan(join_pair, (keep, push), axis=1, reverse=True)
    entering_backward = carried_in(
        (product[:, 0], backward[:, 0]),
        "time",
        join_pair,
        (jnp.ones_like(keep[:, 0]), jnp.zeros_like(push[:, 0])),
    )
    backward = backward + product * entering_backward[1][:, None]
    states = forward + backward
    power = over_axes(jnp.sum(states * states, axis=-1, keepdims=True), CHAN) / (
        states.shape[-1] * lax.axis_size(CHAN)
    )
    mixed_out = (states * lax.rsqrt(power + 1e-06) * norm_gain).astype(jnp.bfloat16)
    return mixed_out


def solution(mesh):
    split = Mesh(mesh.devices.reshape(mesh.shape["time"], 2, 4), ("time", "chan_0", "chan_1"))
    in_specs = (P(None, "time", CHAN), P(None, "time", CHAN), P(CHAN))
    out_specs = P(None, "time", CHAN)
    return jax.shard_map(
        per_device, mesh=split, in_specs=in_specs, out_specs=out_specs, check_vma=False
    )
```

profile of v0, /device:TPU:0, one launch (start us, length us, event | category | flops | bytes accessed | tf_op | source)
XLA Modules:
  0.0 159.9 jit_solution(11750504056960354731)
XLA Ops:
  0.0 1.4 multiply_exponential_fusion
  2.5 2.7 %slice.639 = f32[1,256,512]{2,1,0:T(8,128)} reverse(f32[1,256,512]{2,1,0:T(8,128)S(1)} %slice.548), dimensions={1} | reverse | bytes 1048576 | tf_op jit(solution)/shard_map/slice | solution.py:79
  5.2 2.7 %slice.635 = f32[1,256,512]{2,1,0:T(8,128)} reverse(f32[1,256,512]{2,1,0:T(8,128)S(1)} %slice.552), dimensions={1} | reverse | bytes 1048576 | tf_op jit(solution)/shard_map/slice | solution.py:79
  8.4 2.1 %slice.547 = f32[1,255,512]{2,1,0:T(8,128)} slice(f32[1,512,512]{2,1,0:T(8,128)S(1)} %multiply_exponential_fusion), slice={[0:1:1], [2:512:2], [0:512:1]} | slice | bytes 1044480 | tf_op jit(solution)/shard_map/slice | solution.py:71
  10.5 2.8 %slice.634 = f32[1,255,512]{2,1,0:T(8,128)} reverse(f32[1,255,512]{2,1,0:T(8,128)S(1)} %slice.633), dimensions={1} | reverse | bytes 1044480 | tf_op jit(solution)/shard_map/slice | solution.py:79
  13.5 2.1 %slice.612 = f32[1,255,512]{2,1,0:T(8,128)} slice(f32[1,512,512]{2,1,0:T(8,128)S(1)} %broadcast_multiply_fusion.1), slice={[0:1:1], [2:512:2], [0:512:1]} | slice | bytes 1044480 | tf_op jit(solution)/shard_map/slice | solution.py:71
  22.6 0.9 copy-done.12
  24.0 0.9 add.464
  24.9 0.9 add.454
  26.2 2.3 %pad.237 = f32[1,512,512]{2,1,0:T(8,128)S(1)} pad(f32[1,256,512]{2,1,0:T(8,128)} %add.454, f32[]{:T(128)} %constant.60.clone.1), padding=0_0_0x1_0_1x0_0_0 | pad | bytes 1572868 | tf_op jit(solution)/shard_map/pad | solution.py:71
  28.6 21.2 %all_gather.13 = f32[16,1,512]{2,1,0:T(1,128)S(1)} all-gather(f32[1,1,512]{2,1,0:T(1,128)S(1)} %slice_add_fusion.2), channel_id=1, replica_groups=mesh['time'=16,'chan_0'=2,'chan_1'=4] {'time'}, dimensions={0}, use_global_device_ids=true | all-gather | bytes 34816 | tf_op jit(solution)/shard_map/all_gather | solution.py:12
  49.8 4.7 %pad.255 = f32[1,512,512]{2,1,0:T(8,128)} pad(f32[1,256,512]{2,1,0:T(8,128)} %add.464, f32[]{:T(128)} %constant.60.clone.1), padding=0_0_0x1_0_1x0_0_0 | pad | bytes 1572868 | tf_op jit(solution)/shard_map/pad | solution.py:71
  54.4 0.7 slice_add_fusion.3
  55.2 16.5 %all_gather.12 = f32[16,1,512]{2,1,0:T(1,128)S(1)} all-gather(f32[1,1,512]{2,1,0:T(1,128)S(1)} %slice_add_fusion.3), channel_id=1, replica_groups=mesh['time'=16,'chan_0'=2,'chan_1'=4] {'time'}, dimensions={0}, use_global_device_ids=true | all-gather | bytes 34816 | tf_op jit(solution)/shard_map/all_gather | solution.py:12
  72.3 6.3 %reverse.9 = f32[1,512,512]{2,1,0:T(8,128)S(1)} reverse(bf16[1,512,512]{2,1,0:T(8,128)(2,1)} %param.8), dimensions={1} | reverse | bytes 1572864 | tf_op jit(solution)/shard_map/reverse
  78.8 2.1 %slice.699 = f32[1,255,512]{2,1,0:T(8,128)} slice(f32[1,512,512]{2,1,0:T(8,128)S(1)} %broadcast_multiply_fusion), slice={[0:1:1], [2:512:2], [0:512:1]} | slice | bytes 1044480 | tf_op jit(solution)/shard_map/slice | solution.py:79
  80.9 2.1 %slice.637 = f32[1,256,512]{2,1,0:T(8,128)} slice(f32[1,512,512]{2,1,0:T(8,128)S(1)} %broadcast_multiply_fusion), slice={[0:1:1], [1:512:2], [0:512:1]} | slice | bytes 1048576 | tf_op jit(solution)/shard_map/slice | solution.py:79
  82.9 2.1 %slice.636 = f32[1,256,512]{2,1,0:T(8,128)} slice(f32[1,512,512]{2,1,0:T(8,128)S(1)} %broadcast_multiply_fusion), slice={[0:1:1], [0:511:2], [0:512:1]} | slice | bytes 1048576 | tf_op jit(solution)/shard_map/slice | solution.py:79
  85.0 1.4 fusion.23
  92.1 0.9 copy-done.13
  93.5 0.9 add.490
  94.4 0.9 add.500
  95.7 2.1 %pad.291 = f32[1,512,512]{2,1,0:T(8,128)S(1)} pad(f32[1,256,512]{2,1,0:T(8,128)} %add.500, f32[]{:T(128)} %constant.60.clone.1), padding=0_0_0x1_0_1x0_0_0 | pad | bytes 1572868 | tf_op jit(solution)/shard_map/pad | solution.py:79
  97.8 1.2 add.501
  99.0 8.9 %rev.18 = f32[1,512,512]{2,1,0:T(8,128)} reverse(f32[1,512,512]{2,1,0:T(8,128)} %add.501), dimensions={1} | reverse | bytes 2097152 | tf_op jit(solution)/shard_map/rev | solution.py:79
  108.1 1.2 add.492
  109.3 9.1 %rev.17 = f32[1,512,512]{2,1,0:T(8,128)} reverse(f32[1,512,512]{2,1,0:T(8,128)} %add.492), dimensions={1} | reverse | bytes 2097152 | tf_op jit(solution)/shard_map/rev | solution.py:79
  118.4 17.9 %all-gather.1 = f32[16,2,512]{2,1,0:T(2,128)S(1)} all-gather(f32[1,2,512]{2,1,0:T(2,128)S(1)} %maximum_bitcast_fusion), channel_id=2, replica_groups=mesh['time'=16,'chan_0'=2,'chan_1'=4] {'time'}, dimensions={0}, use_global_device_ids=true | all-gather | bytes 69632 | tf_op jit(solution)/shard_map/all_gather | solution.py:32
  137.0 3.1 %multiply_reduce_fusion = (f32[512]{0:T(512)S(1)}, f32[1,512,512]{2,1,0:T(8,128)}) fusion(f32[1,512,512]{2,1,0:T(8,128)} %rev.17, f32[1,512,512]{2,1,0:T(8,128)} %rev.18, f32[512]{0:T(512)S(1)} %bitcast.34, f32[512]{0:T(512)S(1)} %bitcast.35, f32[1,512,512]{2,1,0:T(8,128)S(1)} %copy-done.1, f32[1,512,512]{2,1,0:T(8,128)} %pad.255, ...), kind=kLoop, calls=%fused_computation.9 | loop fusion | flops 2358784 | bytes 7346176 | tf_op jit(solution)/shard_map/reduce_sum | solution.py:88
  140.2 6.4 %psum.14 = f32[1,512,1]{1,2,0:T(1,128)S(1)} all-reduce(f32[1,512,1]{1,2,0:T(1,128)S(1)} %bitcast.37), channel_id=1, replica_groups=mesh['time'=16,'chan_0'=2,'chan_1'=4] {'chan_0'}, use_global_device_ids=true, to_apply=%region_5.6 | all-reduce | flops 512 | bytes 4096 | tf_op jit(solution)/shard_map/psum | solution.py:59
  146.6 10.5 %psum.15 = f32[1,512,1]{1,2,0:T(1,128)S(1)} all-reduce(f32[1,512,1]{1,2,0:T(1,128)S(1)} %psum.14), channel_id=1, replica_groups=mesh['time'=16,'chan_0'=2,'chan_1'=4] {'chan_1'}, use_global_device_ids=true, to_apply=%region_6.7 | all-reduce | flops 512 | bytes 4096 | tf_op jit(solution)/shard_map/psum | solution.py:59
  157.7 2.2 %multiply_convert_fusion = bf16[1,512,512]{2,1,0:T(8,128)(2,1)} fusion(f32[1,512,512]{2,1,0:T(8,128)} %get-tuple-element.252, f32[512]{0:T(512)S(1)} %copy-done.14, f32[512]{0:T(512)S(1)} %bitcast.36), kind=kLoop, calls=%fused_computation.8 | loop fusion | flops 786432 | bytes 1576960 | tf_op jit(solution)/shard_map/convert_element_type | solution.py:91
  (334 shorter events, 17.7 us)
Async XLA Ops:
  10.5 2.8 %copy-start.6 = (bf16[1,512,512]{2,1,0:T(8,128)(2,1)S(1)}, bf16[1,512,512]{2,1,0:T(8,128)(2,1)}, u32[]{:S(2)}) copy-start(bf16[1,512,512]{2,1,0:T(8,128)(2,1)} %param.8) | copy-start | bytes 1572868
  22.4 1.0 copy-start.12
  22.5 1.1 copy-start.11
  26.1 28.4 %copy-start = (f32[1,512,512]{2,1,0:T(8,128)}, f32[1,512,512]{2,1,0:T(8,128)S(1)}, u32[]{:S(2)}) copy-start(f32[1,512,512]{2,1,0:T(8,128)S(1)} %pad.254) | copy-start | bytes 3145732
  26.2 28.2 %copy-start.2 = (f32[1,512,512]{2,1,0:T(8,128)}, f32[1,512,512]{2,1,0:T(8,128)S(1)}, u32[]{:S(2)}) copy-start(f32[1,512,512]{2,1,0:T(8,128)S(1)} %pad.236) | copy-start | bytes 3145732
  28.6 50.1 %copy-start.4 = (f32[1,512,512]{2,1,0:T(8,128)}, f32[1,512,512]{2,1,0:T(8,128)S(1)}, u32[]{:S(2)}) copy-start(f32[1,512,512]{2,1,0:T(8,128)S(1)} %pad.237) | copy-start | bytes 3145732
  82.9 2.1 %copy-start.8 = (f32[1,256,512]{2,1,0:T(8,128)S(1)}, f32[1,256,512]{2,1,0:T(8,128)}, u32[]{:S(2)}) copy-start(f32[1,256,512]{2,1,0:T(8,128)} %slice.639) | copy-start | bytes 1572868
  82.9 2.1 %copy-start.9 = (f32[1,256,512]{2,1,0:T(8,128)S(1)}, f32[1,256,512]{2,1,0:T(8,128)}, u32[]{:S(2)}) copy-start(f32[1,256,512]{2,1,0:T(8,128)} %slice.635) | copy-start | bytes 1572868
  92.0 1.0 copy-start.13
  92.0 1.1 copy-start.10
  99.0 8.9 %copy-start.7 = (f32[1,256,512]{2,1,0:T(8,128)S(1)}, f32[1,256,512]{2,1,0:T(8,128)}, u32[]{:S(2)}) copy-start(f32[1,256,512]{2,1,0:T(8,128)} %add.490) | copy-start | bytes 1572868
  108.1 28.9 %copy-start.5 = (f32[1,512,512]{2,1,0:T(8,128)S(1)}, f32[1,512,512]{2,1,0:T(8,128)}, u32[]{:S(2)}) copy-start(f32[1,512,512]{2,1,0:T(8,128)} %copy-done.4) | copy-start | bytes 3145732
  109.3 27.7 %copy-start.1 = (f32[1,512,512]{2,1,0:T(8,128)S(1)}, f32[1,512,512]{2,1,0:T(8,128)}, u32[]{:S(2)}) copy-start(f32[1,512,512]{2,1,0:T(8,128)} %copy-done) | copy-start | bytes 3145732
  109.3 27.7 %copy-start.3 = (f32[1,512,512]{2,1,0:T(8,128)S(1)}, f32[1,512,512]{2,1,0:T(8,128)}, u32[]{:S(2)}) copy-start(f32[1,512,512]{2,1,0:T(8,128)} %copy-done.2) | copy-start | bytes 3145732
  157.0 0.7 copy-start.14
where the time goes:
time: 162 us; the launch traced here: 160 us
  blocking collectives  72.5 us (45%)
  local copies, waits for them, and re-layouts  66.5 us (41%)
  other arithmetic  18.4 us (11%)
  between operations  1.76 us (1%)
    all_gather x2, blocking collectives, entering(): pieces = jax.tree.map(lambda part: lax.all_gather(part, axis), value)  37.7 us
    slice x60, local copies, waits for them, and re-layouts, per_device(): lax.associative_scan(join_pair, (keep, push), axis=1, reverse=True)  18.4 us
    rev x2, local copies, waits for them, and re-layouts, per_device(): lax.associative_scan(join_pair, (keep, push), axis=1, reverse=True)  18 us
    all_gather x1, blocking collectives, gathered_once(): both, at, found = (lax.all_gather(jnp.concatenate(lines), axis), 0, {})  17.9 us
    psum x2, blocking collectives, over_axes(): array = lax.psum(array, axis)  16.9 us
    slice x60, local copies, waits for them, and re-layouts, per_device(): product, forward = lax.associative_scan(join_pair, (keep, push), axis=1)  9.83 us
    pad x32, local copies, waits for them, and re-layouts, per_device(): product, forward = lax.associative_scan(join_pair, (keep, push), axis=1)  7.96 us
    another operation x1, local copies, waits for them, and re-layouts  6.26 us

commit v1 on v0

v1 whole, which is shorter than its diff:
```python
import functools

import jax
import jax.numpy as jnp
from jax import lax
from jax.experimental import pallas as pl
from jax.experimental.pallas import tpu as pltpu
from jax.sharding import PartitionSpec as P

LANES = 128
SUBLANES = 8
BLOCK = 256


def dot(a, b):
    return jnp.dot(a, b, preferred_element_type=jnp.float32)


def rows_of(row):
    return [row[:, k : k + LANES] for k in range(0, row.shape[1], LANES)]


def local_kernel(total_length, rate_hbm, update_hbm, gain_hbm, local, fall, rise, stats, send, rate, update, gain, arrived):
    blocks = rate.shape[0] // BLOCK
    count = send.shape[0]
    me = lax.axis_index("time")
    copies = []
    for k in range(blocks):
        span = pl.ds(k * BLOCK, BLOCK)
        copies.append(pltpu.make_async_copy(rate_hbm.at[span], rate.at[span], arrived.at[0, k]))
        copies.append(pltpu.make_async_copy(update_hbm.at[span], update.at[span], arrived.at[1, k]))
    copies.append(pltpu.make_async_copy(gain_hbm, gain, arrived.at[0, blocks]))
    for copy in copies:
        copy.start()
    line = lax.broadcasted_iota(jnp.int32, (BLOCK, BLOCK), 0)
    column = lax.broadcasted_iota(jnp.int32, (BLOCK, BLOCK), 1)
    lower = jnp.where(line >= column, 1.0, 0.0).astype(jnp.bfloat16)
    upper = jnp.where(line <= column, 1.0, 0.0).astype(jnp.bfloat16)
    ends = []
    for k in range(blocks):
        span = pl.ds(k * BLOCK, BLOCK)
        copies[2 * k].wait()
        step = rate[span, :] * (1.0 / total_length)
        high = step.astype(jnp.bfloat16)
        low = (step - high.astype(jnp.float32)).astype(jnp.bfloat16)
        spent = dot(lower, high) + dot(lower, low)
        down = jnp.exp(-spent)
        up = jnp.exp(spent)
        half = 0.5 * step * step
        rising = up * (1.0 - step + half)
        falling = down * (1.0 + step + half)
        copies[2 * k + 1].wait()
        push_half = update[span, :]
        push = push_half.astype(jnp.float32)
        ahead = (up - 1.0) * push
        behind = (falling - 1.0) * push
        ends.append(
            (
                down[BLOCK - 1 :, :],
                down[BLOCK - 1 :, :] * jnp.sum(push + ahead, axis=0, keepdims=True),
                jnp.sum(push + behind, axis=0, keepdims=True),
            )
        )
        earlier = dot(lower, push_half) + dot(lower, ahead.astype(jnp.bfloat16))
        later = dot(upper, push_half) + dot(upper, behind.astype(jnp.bfloat16))
        local[span, :] = down * earlier + rising * later
        fall[span, :] = down
        rise[span, :] = rising
    (keep_0, forward_0, backward_0), (keep_1, forward_1, backward_1) = ends
    keep = keep_0 * keep_1
    forward = keep_1 * forward_0 + forward_1
    backward = backward_0 + keep_0 * backward_1
    copies[-1].wait()
    row = gain[...]
    stats[...] = jnp.concatenate([keep_0, forward_0, keep_1, backward_1, row, row, row, row], axis=0)
    to_later = jnp.concatenate(rows_of(keep) + rows_of(forward), axis=0)
    to_earlier = jnp.concatenate(rows_of(keep) + rows_of(backward), axis=0)
    for peer in range(count):
        send[peer] = jnp.where(peer > me, to_later, to_earlier)


def states_kernel(came, local, fall, rise, stats, states, send):
    count = came.shape[0]
    me = lax.axis_index("time")
    parts = [came[peer] for peer in range(count)]
    ends = [pltpu.roll(part, 4, axis=0) for part in parts]
    before = jnp.zeros((SUBLANES, LANES), jnp.float32)
    after = before
    for k in range(count):
        peer = count - 1 - k
        before = jnp.where(k < me, parts[k] * before + ends[k], before)
        after = jnp.where(peer > me, parts[peer] * after + ends[peer], after)
    before = jnp.concatenate([before[k : k + 1] for k in range(4)], axis=1)
    after = jnp.concatenate([after[k : k + 1] for k in range(4)], axis=1)
    keep_0, forward_0, keep_1, backward_1 = (stats[k : k + 1, :] for k in range(4))
    gain = stats[4:5, :]
    entering = [
        (before, keep_0 * (keep_1 * after + backward_1)),
        (keep_0 * before + forward_0, keep_1 * after),
    ]
    lane = lax.broadcasted_iota(jnp.int32, (SUBLANES, LANES), 1)
    power = jnp.zeros((SUBLANES, LANES), jnp.float32)
    for k in range(local.shape[0] // SUBLANES):
        span = pl.ds(k * SUBLANES, SUBLANES)
        first, second = entering[k * SUBLANES // BLOCK]
        state = local[span, :] + fall[span, :] * first + rise[span, :] * second
        states[span, :] = state * gain
        square = state * state
        square = functools.reduce(jnp.add, rows_of(square))
        power = jnp.where(lane == k, jnp.sum(square, axis=1, keepdims=True), power)
    for peer in range(send.shape[0]):
        send[peer] = power


def norm_kernel(scale, channels, came, states, mixed_hbm, mixed, left):
    power = functools.reduce(jnp.add, [came[peer] for peer in range(came.shape[0])])
    factor = lax.rsqrt(power * (scale * scale / channels) + 1e-6) * scale
    pieces = left.shape[0]
    height = states.shape[0] // pieces
    copies = []
    for piece in range(pieces):
        for k in range(piece * height // 16, (piece + 1) * height // 16):
            halves = []
            for j in (2 * k, 2 * k + 1):
                state = states[pl.ds(j * SUBLANES, SUBLANES), :]
                halves.append(state * factor[:, j : j + 1])
            mixed[pl.ds(16 * k, 16), :] = jnp.concatenate(halves, axis=0).astype(jnp.bfloat16)
        span = pl.ds(piece * height, height)
        copy = pltpu.make_async_copy(mixed.at[span], mixed_hbm.at[span], left.at[piece])
        copy.start()
        copies.append(copy)
    for copy in copies:
        copy.wait()


VMEM = pl.BlockSpec(memory_space=pltpu.VMEM)
HBM = pl.BlockSpec(memory_space=pltpu.HBM)
PARAMS = pltpu.CompilerParams(vmem_limit_bytes=16 << 20)


def placed(space, *arrays):
    return [pltpu.with_memory_space_constraint(array, space) for array in arrays]


def per_device(fade_rate, update_in, norm_gain):
    time, chan = lax.axis_size("time"), lax.axis_size("chan")
    length, width = fade_rate.shape[1:]
    total_length = length * time
    full = pltpu.VMEM((length, width), jnp.float32)
    local, fall, rise, stats, send = pl.pallas_call(
        functools.partial(local_kernel, total_length),
        out_shape=(full, full, full, pltpu.VMEM((SUBLANES, width), jnp.float32), pltpu.VMEM((time, SUBLANES, LANES), jnp.float32)),
        in_specs=[HBM] * 3,
        out_specs=(VMEM,) * 5,
        scratch_shapes=[
            pltpu.VMEM((length, width), jnp.float32),
            pltpu.VMEM((length, width), jnp.bfloat16),
            pltpu.VMEM((1, width), jnp.float32),
            pltpu.SemaphoreType.DMA((2, length // BLOCK + 1)),
        ],
        compiler_params=PARAMS,
        name="local",
    )(*placed(pltpu.HBM, fade_rate[0], update_in[0], norm_gain[None]))
    came = lax.all_to_all(send, "time", 0, 0, tiled=True)
    states, send = pl.pallas_call(
        states_kernel,
        out_shape=(full, pltpu.VMEM((chan, SUBLANES, LANES), jnp.float32)),
        in_specs=[VMEM] * 5,
        out_specs=(VMEM,) * 2,
        compiler_params=PARAMS,
        name="states",
    )(*placed(pltpu.VMEM, came, local, fall, rise, stats))
    came = lax.all_to_all(send, "chan", 0, 0, tiled=True)
    mixed = pl.pallas_call(
        functools.partial(norm_kernel, float(total_length) ** -0.5, width * chan),
        out_shape=jax.ShapeDtypeStruct((length, width), jnp.bfloat16),
        in_specs=[VMEM] * 2,
        out_specs=HBM,
        scratch_shapes=[pltpu.VMEM((length, width), jnp.bfloat16), pltpu.SemaphoreType.DMA((4,))],
        compiler_params=PARAMS,
        name="norm",
    )(*placed(pltpu.VMEM, came, states))
    return mixed[None]


def solution(mesh):
    shard = P(None, "time", "chan")
    return jax.shard_map(
        per_device, mesh=mesh, in_specs=(shard, shard, P("chan")), out_specs=shard, check_vma=False
    )
```

time: 162 us -> 31.4 us (0.19); the launches traced: 160 us -> 31.2 us
  local copies, waits for them, and re-layouts: 66.5 us -> 0 us
  blocking collectives: 72.5 us -> 26.7 us
  other arithmetic: 18.4 us -> 0 us
  Pallas kernels: 0 us -> 4.53 us
  between operations: 1.76 us -> 0.01 us
    all_gather x3 -> x0, blocking collectives: 55.6 us -> none  [the longest x2 37.7 us: entering(): pieces = jax.tree.map(lambda part: lax.all_gather(part, axis), value)]
    slice x121 -> x0, local copies, waits for them, and re-layouts: 28.2 us -> none  [the longest x60 18.4 us: per_device(): lax.associative_scan(join_pair, (keep, push), axis=1, reverse=True)]
    all_to_all x0 -> x2, blocking collectives: none -> 26.7 us  [the longest x1 14.2 us: per_device(): came = lax.all_to_all(send, 'chan', 0, 0, tiled=True)]
    rev x4 -> x0, local copies, waits for them, and re-layouts: 18.1 us -> none  [the longest x2 18 us: per_device(): lax.associative_scan(join_pair, (keep, push), axis=1, reverse=True)]
    psum x2 -> x0, blocking collectives: 16.9 us -> none  [over_axes(): array = lax.psum(array, axis)]
    pad x64 -> x0, local copies, waits for them, and re-layouts: 11.2 us -> none  [the longest x32 7.96 us: per_device(): product, forward = lax.associative_scan(join_pair, (keep, push), axis=1)]
    add x49 -> x0, other arithmetic: 8.05 us -> none  [the longest x17 4.32 us: per_device(): lax.associative_scan(join_pair, (keep, push), axis=1, reverse=True)]
    another operation x1 -> x0, local copies, waits for them, and re-layouts: 6.26 us -> none
where the time goes in v1:
time: 31.4 us; the launch traced here: 31.2 us
  blocking collectives  26.7 us (85%)
  Pallas kernels  4.53 us (14%)
    all_to_all x1, blocking collectives, per_device(): came = lax.all_to_all(send, 'chan', 0, 0, tiled=True)  14.2 us
    all_to_all x1, blocking collectives, per_device(): came = lax.all_to_all(send, 'time', 0, 0, tiled=True)  12.5 us
    pallas_call x1, Pallas kernels, per_device(): pl.pallas_call(functools.partial(local_kernel, total_length), out_shape=(...  3.23 us
    pallas_call x1, Pallas kernels, per_device(): pl.pallas_call(functools.partial(norm_kernel, float(total_length) ** (-0....  0.93 us

profile of v1, /device:TPU:0, one launch (start us, length us, event | category | flops | bytes accessed | tf_op | source)
XLA Modules:
  0.0 31.2 jit_solution(6742241359800345339)
XLA Ops:
  0.0 3.2 %local.1 = (f32[512,512]{1,0:T(8,128)S(1)}, f32[512,512]{1,0:T(8,128)S(1)}, f32[512,512]{1,0:T(8,128)S(1)}, f32[8,512]{1,0:T(8,128)S(1)}, f32[16,8,128]{2,1,0:T(8,128)S(1)}) custom-call(f32[512,512]{1,0:T(8,128)} %bitcast.4, bf16[512,512]{1,0:T(8,128)(2,1)} %bitcast.5, f32[1,512]{1,0:T(1,128)} %bitcast.6), custom_call_target="tpu_custom_call" | custom-call | tf_op jit(solution)/shard_map/local/pallas_call | solution.py:150
  3.2 12.5 %all_to_all.10.came = f32[16,8,128]{2,1,0:T(8,128)S(1)} all-to-all(f32[16,8,128]{2,1,0:T(8,128)S(1)} %get-tuple-element.12), channel_id=1, replica_groups=mesh['time'=16,'chan'=8] {'time'}, dimensions={0} | all-to-all | bytes 131072 | tf_op jit(solution)/shard_map/all_to_all | solution.py:164
  15.7 0.4 %states.1 = (f32[512,512]{1,0:T(8,128)S(1)}, f32[8,8,128]{2,1,0:T(8,128)S(1)}) custom-call(f32[16,8,128]{2,1,0:T(8,128)S(1)} %all_to_all.10.came, f32[512,512]{1,0:T(8,128)S(1)} %get-tuple-element.13.local, f32[512,512]{1,0:T(8,128)S(1)} %get-tuple-element.14.fall, f32[512,512]{1,0:T(8,128)S(1)} %get-tuple-element.15.rise, f32[8,512]{1,0:T(8,128)S(1)} %get-tuple-element.16.stats), custom_call_target="tpu_custom_call" | custom-call | tf_op jit(solution)/shard_map/states/pallas_call | solution.py:165
  16.1 14.2 %all_to_all.11.came = f32[8,8,128]{2,1,0:T(8,128)S(1)} all-to-all(f32[8,8,128]{2,1,0:T(8,128)S(1)} %get-tuple-element.17), channel_id=1, replica_groups=mesh['time'=16,'chan'=8] {'chan'}, dimensions={0} | all-to-all | bytes 65536 | tf_op jit(solution)/shard_map/all_to_all | solution.py:173
  30.3 0.9 %norm.1 = bf16[512,512]{1,0:T(8,128)(2,1)} custom-call(f32[8,8,128]{2,1,0:T(8,128)S(1)} %all_to_all.11.came, f32[512,512]{1,0:T(8,128)S(1)} %get-tuple-element.18.states), custom_call_target="tpu_custom_call" | custom-call | tf_op jit(solution)/shard_map/norm/pallas_call | solution.py:174
